TPU v7x, 32 devices: a whole 2x2x4 slice. The times are simulated.
32 devices in a mesh: row: 8 (over z, y), col: 4 (over x, core).
Axes of the slice: x: 2, y: 2, z: 4, core: 2. Of those that a mesh axis runs over, the one named last changes fastest.
Arguments:
- valence: bfloat16 [32768, 2048], P('row', 'col')
- conduction: bfloat16 [32768, 1024], P('row', 'col')
- point_index: int32 [8192], replicated, may hold values from 0 to 32767, as said below
Outputs:
- gram: float32 [8192, 8192], P('col', 'row')
Inputs may be any that keep to these rules, and one draw needn't show every extreme that they name: `point_index`: 8192 distinct cells; cell g lies in slab g // 4096. In each aligned block of 1024 entries, at most 256 lie in any one slab, and in every block some slab holds exactly 256.
All inputs are finite; a program needn't handle non-finite values.
Results may differ from a plain program's by a relative error of at most 0.0003.
Values may be sent and summed in bfloat16 or wider, within the bound.
A program may use at most 128 MiB of HBM per device.

v0:
```python
import jax
import jax.numpy as jnp
from jax import lax
from jax.sharding import PartitionSpec as P


def broadcast(array, axis, root):
    mine = lax.axis_index(axis) == root
    return lax.psum(jnp.where(mine, array, jnp.zeros_like(array)), axis)


def contract_rows(left, right):
    return lax.dot_general(
        left, right, (((1,), (1,)), ((), ())), preferred_element_type=jnp.float32
    )


def on_device(valence, conduction, point_index):
    row_count = lax.axis_size("row")
    col_count = lax.axis_size("col")
    my_row = lax.axis_index("row")
    grid_cells = valence.shape[0]
    total_points = point_index.shape[0]
    block_points = total_points // row_count
    capacity = max(2 * block_points // row_count, 2)
    blocks = point_index.reshape(row_count, block_points)
    owners = blocks // grid_cells
    offsets = blocks - owners * grid_cells
    onehot = (owners[:, :, None] == jnp.arange(row_count, dtype=jnp.int32)[None, None, :]).astype(
        jnp.int32
    )
    ranks = jnp.sum((jnp.cumsum(onehot, axis=1) - onehot) * onehot, axis=2)
    owned = owners == my_row
    picked = owned[:, None, :] & (
        ranks[:, None, :] == jnp.arange(capacity, dtype=jnp.int32)[None, :, None]
    )
    source_cells = jnp.sum(jnp.where(picked, offsets[:, None, :], 0), axis=2)
    filled = jnp.any(picked, axis=2)[:, :, None]
    send_val = jnp.where(filled, valence[source_cells], 0)
    send_cond = jnp.where(filled, conduction[source_cells], 0)
    got_val, got_cond = (
        lax.all_to_all(send_val, "row", split_axis=0, concat_axis=0, tiled=True),
        lax.all_to_all(send_cond, "row", split_axis=0, concat_axis=0, tiled=True),
    )
    own_owner = lax.dynamic_index_in_dim(owners, my_row, 0, keepdims=False)
    own_rank = lax.dynamic_index_in_dim(ranks, my_row, 0, keepdims=False)
    flat_slot = own_owner * capacity + own_rank
    rows_val = got_val.reshape(row_count * capacity, got_val.shape[2])[flat_slot]
    rows_cond = got_cond.reshape(row_count * capacity, got_cond.shape[2])[flat_slot]
    full_val, full_cond = (
        lax.all_gather(rows_val, "col", axis=1, tiled=True),
        lax.all_gather(rows_cond, "col", axis=1, tiled=True),
    )
    span = row_count // col_count
    first_block = lax.axis_index("col") * span
    pieces_val = []
    pieces_cond = []
    for step in range(span):
        got_block = (
            broadcast(full_val, "row", first_block + step),
            broadcast(full_cond, "row", first_block + step),
        )
        pieces_val.append(got_block[0])
        pieces_cond.append(got_block[1])
    column_val = jnp.concatenate(pieces_val, axis=0)
    column_cond = jnp.concatenate(pieces_cond, axis=0)
    valence_gram = contract_rows(column_val, full_val)
    conduction_gram = contract_rows(column_cond, full_cond)
    return valence_gram * conduction_gram


def solution(mesh):
    placed = (P("row", "col"), P("row", "col"), P())
    return jax.shard_map(
        on_device, mesh=mesh, in_specs=placed, out_specs=P("col", "row"), check_vma=False
    )
```

profile of v0, /device:TPU:0, one launch (start us, length us, event | category | flops | bytes accessed | tf_op | source)
XLA Modules:
  0.0 601.6 jit_solution(13744911776620132198)
XLA Ops:
  6.5 0.9 reshape.150
  7.5 0.8 add_select_fusion
  8.3 18.0 %reduce-window.6 = s32[8,8,8,128]{3,2,1,0:T(8,128)S(1)} reduce-window(s32[8,8,8,128]{3,2,1,0:T(8,128)S(1)} %fusion.15, s32[]{:T(128)} %constant.45.clone.1), window={size=1x1x1x128 pad=0_0x0_0x0_0x127_0}, to_apply=%region_0.1 | reduce-window | flops 8323072 | bytes 524292 | tf_op jit(solution)/shard_map/reduce-window
  26.4 1.2 slice_reduce_fusion
  27.6 1.3 reduce-window.9
  28.9 0.1 broadcast_add_fusion
  29.1 0.1 fusion.14
  29.2 1.3 fusion.5
  30.5 1.8 select_reduce_fusion
  32.3 7.5 %gather_fusion.2 = bf16[2048,256]{1,0:T(8,128)(2,1)S(1)} fusion(bf16[4096,256]{1,0:T(8,128)(2,1)S(1)} %copy-done, s32[2048]{0:T(1024)S(1)} %broadcast_clamp_fusion), kind=kCustom, calls=%fused_computation.2 | custom fusion | bytes 2105344 | tf_op jit(solution)/shard_map/gather | solution.py:40
  39.9 1.3 broadcast_select_fusion.5
  41.1 7.3 %all-to-all-start.1 = ((bf16[8,256,256]{2,1,0:T(8,128)(2,1)}), bf16[8,256,256]{2,1,0:T(8,128)(2,1)S(1)}, u32[]{:S(2)}, u32[]{:S(2)}) async-start(bf16[8,256,256]{2,1,0:T(8,128)(2,1)} %broadcast_select_fusion.5), calls=%async_computation.1 | async-start | bytes 2097152 | tf_op jit(solution)/shard_map/all_to_all | solution.py:43
  48.4 12.0 %gather_fusion = bf16[2048,512]{1,0:T(8,128)(2,1)} fusion(bf16[4096,512]{1,0:T(8,128)(2,1)} %param.3, s32[2048]{0:T(1024)S(1)} %broadcast_clamp_fusion), kind=kCustom, calls=%fused_computation | custom fusion | bytes 4202496 | tf_op jit(solution)/shard_map/gather | solution.py:39
  60.4 2.7 broadcast_select_fusion.4
  63.2 11.0 %all-to-all-done.1 = bf16[8,256,256]{2,1,0:T(8,128)(2,1)S(1)} async-done(((bf16[8,256,256]{2,1,0:T(8,128)(2,1)}), bf16[8,256,256]{2,1,0:T(8,128)(2,1)S(1)}, u32[]{:S(2)}, u32[]{:S(2)}) %all-to-all-start.1) | async-done | bytes 1048608 | tf_op jit(solution)/shard_map/all_to_all | solution.py:43
  74.2 4.3 all-to-all-start
  78.5 0.0 all-gather.7.cloned.1.call-start
  78.6 5.0 gather_fusion.3
  83.6 0.0 all-gather.7.cloned.1.call-update
  83.6 0.0 all-gather.5.cloned.1.call-start
  83.7 42.7 %all-to-all-done = bf16[8,256,512]{2,1,0:T(8,128)(2,1)} async-done(((bf16[8,256,512]{2,1,0:T(8,128)(2,1)}), bf16[8,256,512]{2,1,0:T(8,128)(2,1)}, u32[]{:S(2)}, u32[]{:S(2)}) %all-to-all-start) | async-done | bytes 2097184 | tf_op jit(solution)/shard_map/all_to_all | solution.py:42
  126.3 7.0 %gather_fusion.1 = bf16[1024,512]{1,0:T(8,128)(2,1)} fusion(bf16[2048,512]{1,0:T(8,128)(2,1)} %bitcast.4, s32[1024]{0:T(1024)S(1)} %broadcast_clamp_fusion.1), kind=kCustom, calls=%fused_computation.1 | custom fusion | bytes 2101248 | tf_op jit(solution)/shard_map/gather | solution.py:48
  133.3 0.0 all-gather.5.cloned.1.call-update
  133.3 0.2 all-reduce.3.cloned.1.call-start
  133.6 0.0 all-gather.7.cloned.1.call-done
  133.6 3.9 broadcast_select_fusion.3
  137.5 29.5 %all-gather.5.cloned.1.call-done = bf16[1024,2048]{1,0:T(8,128)(2,1)} async-done(((bf16[1024,512]{1,0:T(8,128)(2,1)}), bf16[1024,2048]{1,0:T(8,128)(2,1)}) %all-gather.5.cloned.1.call-update) | async-done | bytes 4194320 | tf_op jit(solution)/shard_map/all_gather | solution.py:51
  167.0 6.1 %broadcast_select_fusion.1 = (bf16[1024,2048]{1,0:T(8,128)(2,1)}, bf16[1024,2048]{1,0:T(8,128)(2,1)}) fusion(bf16[1024,2048]{1,0:T(8,128)(2,1)} %all-gather.5.cloned.1.call-done, pred[]{:T(512)S(6)} %eq.52, pred[]{:T(512)S(6)} %eq.64), kind=kLoop, calls=%fused_computation.18 | loop fusion | flops 4194304 | bytes 12582914 | tf_op jit(solution)/shard_map/jit(_where)/select_n | solution.py:9
  173.0 0.0 all-reduce.3.cloned.1.call-update
  173.1 394.9 %all-reduce.3.cloned.1.call-done = (bf16[1024,1024]{1,0:T(8,128)(2,1)}, bf16[1024,1024]{1,0:T(8,128)(2,1)}, bf16[1024,2048]{1,0:T(8,128)(2,1)}, bf16[1024,2048]{1,0:T(8,128)(2,1)}) async-done(((bf16[1024,1024]{1,0:T(8,128)(2,1)}, bf16[1024,1024]{1,0:T(8,128)(2,1)}, bf16[1024,2048]{1,0:T(8,128)(2,1)}, bf16[1024,2048]{1,0:T(8,128)(2,1)}), (bf16[1024,1024]{1,0:T(8,128)(2,1)}, bf16[1024,1024]{1,0:T(8,128)(2,1)}, ...) | async-done | bytes 12582928 | tf_op jit(solution)/shard_map/psum | solution.py:9
  568.0 11.0 %fusion.9 = f32[2048,1024]{1,0:T(8,128)} fusion(bf16[1024,1024]{1,0:T(8,128)(2,1)} %all-gather.7.cloned.1.call-done, bf16[1024,1024]{1,0:T(8,128)(2,1)} %get-tuple-element.5, bf16[1024,1024]{1,0:T(8,128)(2,1)} %get-tuple-element.6), kind=kOutput, calls=%fused_computation.13 | convolution fusion | flops 4303355904 | bytes 14680064 | tf_op jit(solution)/shard_map/dot_general | solution.py:13
  579.0 16.1 %fusion.6 = f32[2048,1024]{1,0:T(8,128)} fusion(f32[2048,1024]{1,0:T(8,128)} %fusion.9, bf16[1024,2048]{1,0:T(8,128)(2,1)S(1)} %copy-done.1, bf16[1024,2048]{1,0:T(8,128)(2,1)} %get-tuple-element.7, bf16[1024,2048]{1,0:T(8,128)(2,1)} %get-tuple-element.8), kind=kOutput, calls=%fused_computation.12 | convolution fusion | flops 8608808960 | bytes 29360128 | tf_op jit(solution)/shard_map/dot_general | solution.py:13
  (13 shorter events, 0.2 us)
Async XLA Ops:
  6.5 25.8 %copy-start = (bf16[4096,256]{1,0:T(8,128)(2,1)S(1)}, bf16[4096,256]{1,0:T(8,128)(2,1)}, u32[]{:S(2)}) copy-start(bf16[4096,256]{1,0:T(8,128)(2,1)} %param.4) | copy-start | bytes 6291460
  41.1 33.1 %all-to-all-start.1 = ((bf16[8,256,256]{2,1,0:T(8,128)(2,1)}), bf16[8,256,256]{2,1,0:T(8,128)(2,1)S(1)}, u32[]{:S(2)}, u32[]{:S(2)}) async-start(bf16[8,256,256]{2,1,0:T(8,128)(2,1)} %broadcast_select_fusion.5), calls=%async_computation.1 | async-start | bytes 2097152 | tf_op jit(solution)/shard_map/all_to_all | solution.py:43
  74.2 52.1 %all-to-all-start = ((bf16[8,256,512]{2,1,0:T(8,128)(2,1)}), bf16[8,256,512]{2,1,0:T(8,128)(2,1)}, u32[]{:S(2)}, u32[]{:S(2)}) async-start(bf16[8,256,512]{2,1,0:T(8,128)(2,1)} %broadcast_select_fusion.4), calls=%async_computation | async-start | bytes 4194304 | tf_op jit(solution)/shard_map/all_to_all | solution.py:42
  78.5 55.0 %all-gather.7.cloned.1.call-start = ((), (), s32[]{:S(2)}) async-start(), calls=%async_computation.3 | async-start | bytes 2621440 | tf_op jit(solution)/shard_map/all_gather | solution.py:52
  83.6 83.4 %all-gather.5.cloned.1.call-start = ((), (), s32[]{:S(2)}) async-start(), calls=%async_computation.2 | async-start | bytes 5242880 | tf_op jit(solution)/shard_map/all_gather | solution.py:51
  133.3 434.7 %all-reduce.3.cloned.1.call-start = ((), (), s32[]{:S(2)}) async-start(), calls=%async_computation.4 | async-start | bytes 25165824 | tf_op jit(solution)/shard_map/psum | solution.py:9
  568.0 11.0 %copy-start.1 = (bf16[1024,2048]{1,0:T(8,128)(2,1)S(1)}, bf16[1024,2048]{1,0:T(8,128)(2,1)}, u32[]{:S(2)}) copy-start(bf16[1024,2048]{1,0:T(8,128)(2,1)} %all-gather.5.cloned.1.call-done) | copy-start | bytes 12582916
Sparse Core Ops, SparseCore 0:
  83.7 24.0 all-gather.6
  133.4 33.4 all-gather.4
  173.2 394.7 all-reduce.2
where the time goes:
time: 602 us
  waiting for transfers between devices  478 us (79%)
  other arithmetic  37.5 us (6%)
  local copies, waits for them, and re-layouts  33.6 us (6%)
  matrix products  27.1 us (5%)
  between operations  13.3 us (2%)
  starting transfers between devices  12 us (2%)
    psum x1, waiting for transfers between devices, broadcast(): return lax.psum(jnp.where(mine, array, jnp.zeros_like(array)), axis)  395 us
    all_to_all x1, waiting for transfers between devices, on_device(): lax.all_to_all(send_val, 'row', split_axis=0, concat_axis=0, tiled=True)  42.7 us
    all_gather x1, waiting for transfers between devices, on_device(): lax.all_gather(rows_val, 'col', axis=1, tiled=True)  29.5 us
    dot_general x2, matrix products, contract_rows(): lax.dot_general(left, right, (((1,), (1,)), ((), ())), preferred_element_...  27.1 us
    another operation x3, other arithmetic  19.4 us
  transfers between devices with their start and end apart: 5, of which 4 were waited for; matrix products, arithmetic and copies ran while one was open for 5% of the time, Pallas kernels for 0%

commit v1 on v0

v1 whole, which is shorter than its diff:
```python
import functools

import jax
import jax.numpy as jnp
from jax import lax
from jax.experimental import pallas as pl
from jax.experimental.pallas import tpu as pltpu
from jax.sharding import PartitionSpec as P

MESH = pl.DeviceIdType.MESH
CHUNK_ROWS = 16
GROUP = 8
COLUMN_TILE = 256


def spread_kernel(
    n, c, wv, w, half,
    x_ref, o_ref, own, full, own_sem, peer_send, peer_recv, mate_send, mate_recv, ring_send, ring_recv,
):
    span = n // c
    pairs = c // 2
    chunks = half // CHUNK_ROWS
    stage_rows = half // GROUP
    group_rows = GROUP * CHUNK_ROWS
    row, col = lax.axis_index("row"), lax.axis_index("col")
    core, chip = lax.rem(col, 2), col // 2
    mate = chip * 2 + 1 - core

    def position(r):
        y, z = lax.rem(r, 2), r // 2
        return (1 - y) * z + y * (n - 1 - z)

    def row_at(p):
        back = p // (n // 2)
        return (1 - back) * (2 * p) + back * (2 * (n - 1 - p) + 1)

    here = position(row)
    right, left = row_at(lax.rem(here + 1, n)), row_at(lax.rem(here + n - 1, n))

    barrier = pltpu.get_barrier_semaphore()
    for other in (left, right):
        pl.semaphore_signal(barrier, inc=1, device_id=(other, col), device_id_type=MESH)
    for q in range(1, c):
        pl.semaphore_signal(
            barrier, inc=1, device_id=(row, lax.rem(col + q, c)), device_id_type=MESH
        )

    def piece(owner, first, count):
        return own.at[pl.ds(first, count), pl.ds(pl.multiple_of(owner * w, 128), w)]

    mine = pltpu.make_async_copy(x_ref, piece(col, 0, 2 * half), own_sem)
    mine.start()
    pl.semaphore_wait(barrier, 2 + c - 1)
    mine.wait()

    def stage_first(m, h):
        return pl.multiple_of(h * half + m * stage_rows, stage_rows)

    def to_peer(q, owner, m, h):
        ref = piece(owner, stage_first(m, h), stage_rows)
        return pltpu.make_async_remote_copy(
            src_ref=ref, dst_ref=ref,
            send_sem=peer_send.at[q - 1], recv_sem=peer_recv.at[q - 1, m, h],
            device_id=(row, lax.rem(chip + q, pairs) * 2 + core), device_id_type=MESH,
        )

    def to_mate(q, owner, m, h):
        ref = piece(owner, stage_first(m, h), stage_rows)
        return pltpu.make_async_remote_copy(
            src_ref=ref, dst_ref=ref,
            send_sem=mate_send.at[q], recv_sem=mate_recv.at[q, m, h],
            device_id=(row, mate), device_id_type=MESH,
        )

    def send_own(m, _):
        for h in range(2):
            for q in range(1, pairs):
                to_peer(q, col, m, h).start()
            to_mate(0, col, m, h).start()
        return 0

    lax.fori_loop(0, GROUP, send_own, 0)

    def stream(i, t):
        s, back = i // 2, lax.rem(i, 2)
        source = position(span * col + s)
        distance = lax.rem((1 - back) * (here - source) + back * (source - here) + n, n)
        return s, back, distance, t - distance

    def ring_copy(i, k, s, back, source_ref, source_first):
        first = pl.multiple_of(s * 2 * half + back * half + k * CHUNK_ROWS, CHUNK_ROWS)
        return pltpu.make_async_remote_copy(
            src_ref=source_ref.at[pl.ds(pl.multiple_of(source_first, CHUNK_ROWS), CHUNK_ROWS)],
            dst_ref=full.at[pl.ds(first, CHUNK_ROWS)],
            send_sem=ring_send.at[i], recv_sem=ring_recv.at[i, k],
            device_id=((1 - back) * right + back * left, col), device_id_type=MESH,
        )

    def step(t, _):
        @pl.when(t < GROUP)
        def _():
            for h in range(2):
                for q in range(1, pairs):
                    owner = lax.rem(chip - q + pairs, pairs) * 2 + core
                    to_peer(q, owner, t, h).wait_recv()
                    to_mate(q, owner, t, h).start()
            for h in range(2):
                for q in range(pairs):
                    owner = lax.rem(chip - q + pairs, pairs) * 2 + 1 - core
                    to_mate(q, owner, t, h).wait_recv()

        def forward(i, _):
            s, back, distance, k = stream(i, t)

            @pl.when((k >= 0) & (k < chunks))
            def _():
                in_block = back * half + k * CHUNK_ROWS

                @pl.when(distance == 0)
                def _():
                    ring_copy(i, k, s, back, own, in_block).start()

                @pl.when(distance > 0)
                def _():
                    copy = ring_copy(i, k, s, back, full, s * 2 * half + in_block)
                    copy.wait_recv()

                    @pl.when(distance < n - 1)
                    def _():
                        copy.start()

            return 0

        lax.fori_loop(0, 2 * span, forward, 0)

        def compute(i, _):
            s, back, distance, k = stream(i, t)

            @pl.when((k >= 0) & (k < chunks) & (lax.rem(k + GROUP, GROUP) == GROUP - 1))
            def _():
                in_block = pl.multiple_of(
                    back * half + (k - (GROUP - 1)) * CHUNK_ROWS, group_rows
                )
                first = pl.multiple_of(s * 2 * half + in_block, group_rows)

                @pl.when(distance == 0)
                def _():
                    full[pl.ds(first, group_rows), :] = own[pl.ds(in_block, group_rows), :]

                def tile(j, _):
                    begin = pl.multiple_of(j * COLUMN_TILE, COLUMN_TILE)
                    totals = []
                    for low, high in ((0, wv), (wv, w)):
                        total = None
                        for p in range(c):
                            part = lax.dot_general(
                                full[pl.ds(first, group_rows), p * w + low : p * w + high],
                                own[pl.ds(begin, COLUMN_TILE), p * w + low : p * w + high],
                                (((1,), (1,)), ((), ())),
                                preferred_element_type=jnp.float32,
                            )
                            total = part if total is None else total + part
                        totals.append(total)
                    o_ref[pl.ds(first, group_rows), pl.ds(begin, COLUMN_TILE)] = totals[0] * totals[1]
                    return 0

                lax.fori_loop(0, 2 * half // COLUMN_TILE, tile, 0)

            return 0

        lax.fori_loop(0, 2 * span, compute, 0)
        return 0

    lax.fori_loop(0, chunks + n - 1, step, 0)

    whole = piece(col, 0, 2 * half)
    for q in range(pairs):
        if q >= 1:
            pltpu.make_async_copy(whole, whole, peer_send.at[q - 1]).wait()
        pltpu.make_async_copy(whole, whole, mate_send.at[q]).wait()

    def drain(i, _):
        distance = stream(i, 0)[2]

        @pl.when(distance < n - 1)
        def _():
            stretch = full.at[pl.ds(0, half)]
            pltpu.make_async_copy(stretch, stretch, ring_send.at[i]).wait()

        return 0

    lax.fori_loop(0, 2 * span, drain, 0)


def spread_and_multiply(x, wv, n, c):
    points, w = x.shape
    span = n // c
    half = points // 2
    chunks = half // CHUNK_ROWS
    pairs = c // 2
    return pl.pallas_call(
        functools.partial(spread_kernel, n, c, wv, w, half),
        out_shape=jax.ShapeDtypeStruct((span * points, points), jnp.float32),
        in_specs=[pl.BlockSpec(memory_space=pl.ANY)],
        out_specs=pl.BlockSpec(memory_space=pltpu.VMEM),
        scratch_shapes=[
            pltpu.VMEM((points, c * w), jnp.bfloat16),
            pltpu.VMEM((span * points, c * w), jnp.bfloat16),
            pltpu.SemaphoreType.DMA,
            pltpu.SemaphoreType.DMA((max(pairs - 1, 1),)),
            pltpu.SemaphoreType.DMA((max(pairs - 1, 1), GROUP, 2)),
            pltpu.SemaphoreType.DMA((pairs,)),
            pltpu.SemaphoreType.DMA((pairs, GROUP, 2)),
            pltpu.SemaphoreType.DMA((2 * span,)),
            pltpu.SemaphoreType.DMA((2 * span, chunks)),
        ],
        compiler_params=pltpu.CompilerParams(
            collective_id=0, has_side_effects=True, vmem_limit_bytes=48 * 1024 * 1024
        ),
    )(x)


def on_device(valence, conduction, point_index):
    row_count = lax.axis_size("row")
    col_count = lax.axis_size("col")
    my_row = lax.axis_index("row")
    grid_cells = valence.shape[0]
    total_points = point_index.shape[0]
    block_points = total_points // row_count
    capacity = max(2 * block_points // row_count, 2)
    blocks = point_index.reshape(row_count, block_points)
    owners = blocks // grid_cells
    offsets = blocks - owners * grid_cells
    onehot = owners[:, None, :] == jnp.arange(row_count, dtype=jnp.int32)[None, :, None]
    place = jnp.arange(block_points, dtype=jnp.int32)
    earlier = (place[:, None] < place[None, :]).astype(jnp.bfloat16)
    before = lax.dot_general(
        onehot.astype(jnp.bfloat16), earlier, (((2,), (0,)), ((), ())),
        preferred_element_type=jnp.float32,
    )
    ranks = jnp.sum(jnp.where(onehot, before, 0.0), axis=1).astype(jnp.int32)
    owned = owners == my_row
    picked = owned[:, None, :] & (
        ranks[:, None, :] == jnp.arange(capacity, dtype=jnp.int32)[None, :, None]
    )
    source_cells = jnp.sum(jnp.where(picked, offsets[:, None, :], 0), axis=2)
    own_owner = lax.dynamic_index_in_dim(owners, my_row, 0, keepdims=False)
    own_rank = lax.dynamic_index_in_dim(ranks, my_row, 0, keepdims=False)
    flat_slot = own_owner * capacity + own_rank

    def route(array):
        send = array.at[source_cells].get(mode="promise_in_bounds")
        got = lax.all_to_all(send, "row", split_axis=0, concat_axis=0, tiled=True)
        got = got.reshape(row_count * capacity, got.shape[2])
        return got.at[flat_slot].get(mode="promise_in_bounds")

    rows = jnp.concatenate([route(valence), route(conduction)], axis=1)
    return spread_and_multiply(rows, valence.shape[1], row_count, col_count)


def solution(mesh):
    placed = (P("row", "col"), P("row", "col"), P())
    return jax.shard_map(
        on_device, mesh=mesh, in_specs=placed, out_specs=P("col", "row"), check_vma=False
    )
```

time: 602 us -> 305 us (0.51)
  waiting for transfers between devices: 478 us -> 56.5 us
  Pallas kernels: 0 us -> 191 us
  other arithmetic: 37.5 us -> 3.07 us
  matrix products: 27.1 us -> 0.4 us
  between operations: 13.3 us -> 0.1 us
  local copies, waits for them, and re-layouts: 33.6 us -> 41.2 us
    psum x1 -> x0, waiting for transfers between devices: 395 us -> none  [broadcast(): return lax.psum(jnp.where(mine, array, jnp.zeros_like(array)), axis)]
    pallas_call x0 -> x1, Pallas kernels: none -> 191 us  [spread_and_multiply(): pl.pallas_call(functools.partial(spread_kernel, n, c, wv, w, half), out_s...]
    all_gather x2 -> x0, waiting for transfers between devices: 29.5 us -> none  [the longest x1 29.5 us: on_device(): lax.all_gather(rows_val, 'col', axis=1, tiled=True)]
    dot_general x2 -> x1, matrix products: 27.1 us -> 0.4 us  [on_device(): lax.dot_general(onehot.astype(jnp.bfloat16), earlier, (((2,), (0,)), ((),...]
    another operation x3 -> x0, other arithmetic: 19.4 us -> none
    select_n x5 -> x1, other arithmetic: 14 us -> 0.02 us  [route(): return got.at[flat_slot].get(mode='promise_in_bounds')]
    unnamed x5 -> x4, local copies, waits for them, and re-layouts: 0.01 us -> 8.45 us
  transfers between devices with their start and end apart: 5 -> 2, of which waited for: 4 -> 2; matrix products, arithmetic and copies ran while one was open for 5% -> 6% of each run, Pallas kernels for 0% -> 0%
where the time goes in v1:
time: 305 us; the launch traced here: 304 us
  Pallas kernels  191 us (63%)
  waiting for transfers between devices  56.5 us (19%)
  local copies, waits for them, and re-layouts  41.2 us (14%)
  starting transfers between devices  11.7 us (4%)
  other arithmetic  3.07 us (1%)
    pallas_call x1, Pallas kernels, spread_and_multiply(): pl.pallas_call(functools.partial(spread_kernel, n, c, wv, w, half), out_s...  191 us
    all_to_all x2, waiting for transfers between devices, route(): got = lax.all_to_all(send, 'row', split_axis=0, concat_axis=0, tiled=True)  56.5 us
    gather x2, local copies, waits for them, and re-layouts, route(): send = array.at[source_cells].get(mode='promise_in_bounds')  21 us
    all_to_all x2, starting transfers between devices, route(): got = lax.all_to_all(send, 'row', split_axis=0, concat_axis=0, tiled=True)  11.7 us
    gather x2, local copies, waits for them, and re-layouts, route(): return got.at[flat_slot].get(mode='promise_in_bounds')  10.8 us
    unnamed x4, local copies, waits for them, and re-layouts  8.45 us
  transfers between devices with their start and end apart: 2, of which 2 were waited for; matrix products, arithmetic and copies ran while one was open for 6% of the time, Pallas kernels for 0%

profile of v1, /device:TPU:0, one launch (start us, length us, event | category | flops | bytes accessed | tf_op | source)
XLA Modules:
  0.0 304.3 jit_solution(11731345287739410962)
XLA Ops:
  0.0 0.0 copy-start
  0.0 0.9 reshape.109
  1.0 0.4 fusion.7
  1.4 1.8 select_reduce_fusion
  3.3 0.0 copy-done
  3.3 9.0 %gather_fusion.2 = bf16[2048,256]{1,0:T(8,128)(2,1)} fusion(bf16[4096,256]{1,0:T(8,128)(2,1)S(1)} %copy-done, s32[2048]{0:T(1024)S(1)} %broadcast_clamp_fusion), kind=kCustom, calls=%fused_computation.2 | custom fusion | bytes 2105344 | tf_op jit(solution)/shard_map/gather | solution.py:252
  12.3 7.3 %all-to-all-start.1 = ((bf16[8,256,256]{2,1,0:T(8,128)(2,1)}), bf16[8,256,256]{2,1,0:T(8,128)(2,1)S(1)}, u32[]{:S(2)}, u32[]{:S(2)}) async-start(bf16[8,256,256]{2,1,0:T(8,128)(2,1)} %bitcast.22), calls=%async_computation.1 | async-start | bytes 2097152 | tf_op jit(solution)/shard_map/all_to_all | solution.py:253
  19.6 12.0 %gather_fusion = bf16[2048,512]{1,0:T(8,128)(2,1)} fusion(bf16[4096,512]{1,0:T(8,128)(2,1)} %param.3, s32[2048]{0:T(1024)S(1)} %broadcast_clamp_fusion), kind=kCustom, calls=%fused_computation | custom fusion | bytes 4202496 | tf_op jit(solution)/shard_map/gather | solution.py:252
  31.6 13.8 %all-to-all-done.1 = bf16[8,256,256]{2,1,0:T(8,128)(2,1)S(1)} async-done(((bf16[8,256,256]{2,1,0:T(8,128)(2,1)}), bf16[8,256,256]{2,1,0:T(8,128)(2,1)S(1)}, u32[]{:S(2)}, u32[]{:S(2)}) %all-to-all-start.1) | async-done | bytes 1048608 | tf_op jit(solution)/shard_map/all_to_all | solution.py:253
  45.4 4.3 %all-to-all-start = ((bf16[8,256,512]{2,1,0:T(8,128)(2,1)}), bf16[8,256,512]{2,1,0:T(8,128)(2,1)}, u32[]{:S(2)}, u32[]{:S(2)}) async-start(bf16[8,256,512]{2,1,0:T(8,128)(2,1)} %bitcast.21), calls=%async_computation | async-start | bytes 4194304 | tf_op jit(solution)/shard_map/all_to_all | solution.py:253
  49.8 5.0 %gather_fusion.3 = bf16[1024,256]{1,0:T(8,128)(2,1)} fusion(bf16[2048,256]{1,0:T(8,128)(2,1)S(1)} %bitcast.20, s32[1024]{0:T(1024)S(1)} %broadcast_clamp_fusion.1), kind=kCustom, calls=%fused_computation.3 | custom fusion | bytes 1052672 | tf_op jit(solution)/shard_map/gather | solution.py:255
  54.8 42.8 %all-to-all-done = bf16[8,256,512]{2,1,0:T(8,128)(2,1)} async-done(((bf16[8,256,512]{2,1,0:T(8,128)(2,1)}), bf16[8,256,512]{2,1,0:T(8,128)(2,1)}, u32[]{:S(2)}, u32[]{:S(2)}) %all-to-all-start) | async-done | bytes 2097184 | tf_op jit(solution)/shard_map/all_to_all | solution.py:253
  97.5 5.8 %gather_fusion.1 = bf16[1024,512]{1,0:T(8,128)(2,1)S(1)} fusion(bf16[2048,512]{1,0:T(8,128)(2,1)} %bitcast.3, s32[1024]{0:T(1024)S(1)} %broadcast_clamp_fusion.1), kind=kCustom, calls=%fused_computation.1 | custom fusion | bytes 2101248 | tf_op jit(solution)/shard_map/gather | solution.py:255
  103.4 1.1 pad_maximum_fusion.x_ref
  104.5 191.3 %shard_map.37 = f32[2048,1024]{1,0:T(8,128)} custom-call(bf16[1024,768]{1,0:T(8,128)(2,1)S(1)} %pad_maximum_fusion.x_ref), custom_call_target="tpu_custom_call" | custom-call | tf_op jit(solution)/shard_map/pallas_call | solution.py:201
  295.8 8.4 %copy.6 = f32[2048,1024]{1,0:T(8,128)} copy(f32[2048,1024]{1,0:T(8,128)} %shard_map.37) | data formatting | bytes 16777216
  (8 shorter events, 0.1 us)
Async XLA Ops:
  0.0 3.3 %copy-start = (bf16[4096,256]{1,0:T(8,128)(2,1)S(1)}, bf16[4096,256]{1,0:T(8,128)(2,1)}, u32[]{:S(2)}) copy-start(bf16[4096,256]{1,0:T(8,128)(2,1)} %param.4) | copy-start | bytes 6291460
  12.3 33.1 %all-to-all-start.1 = ((bf16[8,256,256]{2,1,0:T(8,128)(2,1)}), bf16[8,256,256]{2,1,0:T(8,128)(2,1)S(1)}, u32[]{:S(2)}, u32[]{:S(2)}) async-start(bf16[8,256,256]{2,1,0:T(8,128)(2,1)} %bitcast.22), calls=%async_computation.1 | async-start | bytes 2097152 | tf_op jit(solution)/shard_map/all_to_all | solution.py:253
  45.4 52.1 %all-to-all-start = ((bf16[8,256,512]{2,1,0:T(8,128)(2,1)}), bf16[8,256,512]{2,1,0:T(8,128)(2,1)}, u32[]{:S(2)}, u32[]{:S(2)}) async-start(bf16[8,256,512]{2,1,0:T(8,128)(2,1)} %bitcast.21), calls=%async_computation | async-start | bytes 4194304 | tf_op jit(solution)/shard_map/all_to_all | solution.py:253

commit v2 on v1

--- a/solution.py
+++ b/solution.py
@@ -22,6 +22,7 @@
     chunks = half // CHUNK_ROWS
     stage_rows = half // GROUP
     group_rows = GROUP * CHUNK_ROWS
+    stride = GROUP // (2 * half // COLUMN_TILE)
     row, col = lax.axis_index("row"), lax.axis_index("col")
     core, chip = lax.rem(col, 2), col // 2
     mate = chip * 2 + 1 - core
@@ -135,43 +136,39 @@
 
         def compute(i, _):
             s, back, distance, k = stream(i, t)
-
-            @pl.when((k >= 0) & (k < chunks) & (lax.rem(k + GROUP, GROUP) == GROUP - 1))
+            since = k - (GROUP - 1)
+            phase = lax.rem(since + GROUP, GROUP)
+
+            @pl.when((since >= 0) & (since < chunks) & (lax.rem(phase, stride) == 0))
             def _():
-                in_block = pl.multiple_of(
-                    back * half + (k - (GROUP - 1)) * CHUNK_ROWS, group_rows
-                )
+                in_block = pl.multiple_of(back * half + (since - phase) * CHUNK_ROWS, group_rows)
                 first = pl.multiple_of(s * 2 * half + in_block, group_rows)
-
-                @pl.when(distance == 0)
+                begin = pl.multiple_of(phase // stride * COLUMN_TILE, COLUMN_TILE)
+
+                @pl.when((distance == 0) & (phase == 0))
                 def _():
                     full[pl.ds(first, group_rows), :] = own[pl.ds(in_block, group_rows), :]
 
-                def tile(j, _):
-                    begin = pl.multiple_of(j * COLUMN_TILE, COLUMN_TILE)
-                    totals = []
-                    for low, high in ((0, wv), (wv, w)):
-                        total = None
-                        for p in range(c):
-                            part = lax.dot_general(
-                                full[pl.ds(first, group_rows), p * w + low : p * w + high],
-                                own[pl.ds(begin, COLUMN_TILE), p * w + low : p * w + high],
-                                (((1,), (1,)), ((), ())),
-                                preferred_element_type=jnp.float32,
-                            )
-                            total = part if total is None else total + part
-                        totals.append(total)
-                    o_ref[pl.ds(first, group_rows), pl.ds(begin, COLUMN_TILE)] = totals[0] * totals[1]
-                    return 0
-
-                lax.fori_loop(0, 2 * half // COLUMN_TILE, tile, 0)
+                totals = []
+                for low, high in ((0, wv), (wv, w)):
+                    total = None
+                    for p in range(c):
+                        part = lax.dot_general(
+                            full[pl.ds(first, group_rows), p * w + low : p * w + high],
+                            own[pl.ds(begin, COLUMN_TILE), p * w + low : p * w + high],
+                            (((1,), (1,)), ((), ())),
+                            preferred_element_type=jnp.float32,
+                        )
+                        total = part if total is None else total + part
+                    totals.append(total)
+                o_ref[pl.ds(first, group_rows), pl.ds(begin, COLUMN_TILE)] = totals[0] * totals[1]
 
             return 0
 
         lax.fori_loop(0, 2 * span, compute, 0)
         return 0
 
-    lax.fori_loop(0, chunks + n - 1, step, 0)
+    lax.fori_loop(0, chunks + n - 1 + GROUP - 1, step, 0)
 
     whole = piece(col, 0, 2 * half)
     for q in range(pairs):
@@ -200,7 +197,7 @@
     pairs = c // 2
     return pl.pallas_call(
         functools.partial(spread_kernel, n, c, wv, w, half),
-        out_shape=jax.ShapeDtypeStruct((span * points, points), jnp.float32),
+        out_shape=pltpu.VMEM((span * points, points), jnp.float32),
         in_specs=[pl.BlockSpec(memory_space=pl.ANY)],
         out_specs=pl.BlockSpec(memory_space=pltpu.VMEM),
         scratch_shapes=[
@@ -215,7 +212,7 @@
             pltpu.SemaphoreType.DMA((2 * span, chunks)),
         ],
         compiler_params=pltpu.CompilerParams(
-            collective_id=0, has_side_effects=True, vmem_limit_bytes=48 * 1024 * 1024
+            collective_id=0, has_side_effects=True, vmem_limit_bytes=32 * 1024 * 1024
         ),
     )(x)
 

time: 305 us -> 290 us (0.951)
  Pallas kernels: 191 us -> 180 us
  local copies, waits for them, and re-layouts: 41.2 us -> 36.2 us
    pallas_call x1, Pallas kernels: 191 us -> 180 us  [spread_and_multiply(): pl.pallas_call(functools.partial(spread_kernel, n, c, wv, w, half), out_s...]
    unnamed x4, local copies, waits for them, and re-layouts: 8.45 us -> 3.41 us
where the time goes in v2:
time: 290 us; the launch traced here: 288 us
  Pallas kernels  180 us (62%)
  waiting for transfers between devices  56.5 us (19%)
  local copies, waits for them, and re-layouts  36.2 us (12%)
  starting transfers between devices  11.7 us (4%)
  other arithmetic  3.07 us (1%)
    pallas_call x1, Pallas kernels, spread_and_multiply(): pl.pallas_call(functools.partial(spread_kernel, n, c, wv, w, half), out_s...  180 us
    all_to_all x2, waiting for transfers between devices, route(): got = lax.all_to_all(send, 'row', split_axis=0, concat_axis=0, tiled=True)  56.5 us
    gather x2, local copies, waits for them, and re-layouts, route(): send = array.at[source_cells].get(mode='promise_in_bounds')  21 us
    all_to_all x2, starting transfers between devices, route(): got = lax.all_to_all(send, 'row', split_axis=0, concat_axis=0, tiled=True)  11.7 us
    gather x2, local copies, waits for them, and re-layouts, route(): return got.at[flat_slot].get(mode='promise_in_bounds')  10.8 us
  transfers between devices with their start and end apart: 2, of which 2 were waited for; matrix products, arithmetic and copies ran while one was open for 6% of the time, Pallas kernels for 0%

profile of v2, /device:TPU:0, one launch (start us, length us, event | category | flops | bytes accessed | tf_op | source)
XLA Modules:
  0.0 288.2 jit_solution(3225002251953019800)
XLA Ops:
  0.0 0.0 copy-start
  0.0 0.9 reshape.109
  1.0 0.4 fusion.7
  1.4 1.8 select_reduce_fusion
  3.3 0.0 copy-done
  3.3 9.0 %gather_fusion.2 = bf16[2048,256]{1,0:T(8,128)(2,1)} fusion(bf16[4096,256]{1,0:T(8,128)(2,1)S(1)} %copy-done, s32[2048]{0:T(1024)S(1)} %broadcast_clamp_fusion), kind=kCustom, calls=%fused_computation.2 | custom fusion | bytes 2105344 | tf_op jit(solution)/shard_map/gather | solution.py:249
  12.3 7.3 %all-to-all-start.1 = ((bf16[8,256,256]{2,1,0:T(8,128)(2,1)}), bf16[8,256,256]{2,1,0:T(8,128)(2,1)S(1)}, u32[]{:S(2)}, u32[]{:S(2)}) async-start(bf16[8,256,256]{2,1,0:T(8,128)(2,1)} %bitcast.22), calls=%async_computation.1 | async-start | bytes 2097152 | tf_op jit(solution)/shard_map/all_to_all | solution.py:250
  19.6 12.0 %gather_fusion = bf16[2048,512]{1,0:T(8,128)(2,1)} fusion(bf16[4096,512]{1,0:T(8,128)(2,1)} %param.3, s32[2048]{0:T(1024)S(1)} %broadcast_clamp_fusion), kind=kCustom, calls=%fused_computation | custom fusion | bytes 4202496 | tf_op jit(solution)/shard_map/gather | solution.py:249
  31.6 13.8 %all-to-all-done.1 = bf16[8,256,256]{2,1,0:T(8,128)(2,1)S(1)} async-done(((bf16[8,256,256]{2,1,0:T(8,128)(2,1)}), bf16[8,256,256]{2,1,0:T(8,128)(2,1)S(1)}, u32[]{:S(2)}, u32[]{:S(2)}) %all-to-all-start.1) | async-done | bytes 1048608 | tf_op jit(solution)/shard_map/all_to_all | solution.py:250
  45.4 4.3 %all-to-all-start = ((bf16[8,256,512]{2,1,0:T(8,128)(2,1)}), bf16[8,256,512]{2,1,0:T(8,128)(2,1)}, u32[]{:S(2)}, u32[]{:S(2)}) async-start(bf16[8,256,512]{2,1,0:T(8,128)(2,1)} %bitcast.21), calls=%async_computation | async-start | bytes 4194304 | tf_op jit(solution)/shard_map/all_to_all | solution.py:250
  49.8 5.0 %gather_fusion.3 = bf16[1024,256]{1,0:T(8,128)(2,1)} fusion(bf16[2048,256]{1,0:T(8,128)(2,1)S(1)} %bitcast.20, s32[1024]{0:T(1024)S(1)} %broadcast_clamp_fusion.1), kind=kCustom, calls=%fused_computation.3 | custom fusion | bytes 1052672 | tf_op jit(solution)/shard_map/gather | solution.py:252
  54.8 42.8 %all-to-all-done = bf16[8,256,512]{2,1,0:T(8,128)(2,1)} async-done(((bf16[8,256,512]{2,1,0:T(8,128)(2,1)}), bf16[8,256,512]{2,1,0:T(8,128)(2,1)}, u32[]{:S(2)}, u32[]{:S(2)}) %all-to-all-start) | async-done | bytes 2097184 | tf_op jit(solution)/shard_map/all_to_all | solution.py:250
  97.5 5.8 %gather_fusion.1 = bf16[1024,512]{1,0:T(8,128)(2,1)S(1)} fusion(bf16[2048,512]{1,0:T(8,128)(2,1)} %bitcast.3, s32[1024]{0:T(1024)S(1)} %broadcast_clamp_fusion.1), kind=kCustom, calls=%fused_computation.1 | custom fusion | bytes 2101248 | tf_op jit(solution)/shard_map/gather | solution.py:252
  103.4 1.1 pad_maximum_fusion.x_ref
  104.5 180.3 %shard_map.37 = f32[2048,1024]{1,0:T(8,128)S(1)} custom-call(bf16[1024,768]{1,0:T(8,128)(2,1)S(1)} %pad_maximum_fusion.x_ref), custom_call_target="tpu_custom_call" | custom-call | tf_op jit(solution)/shard_map/pallas_call | solution.py:198
  284.8 3.4 %copy.6 = f32[2048,1024]{1,0:T(8,128)} copy(f32[2048,1024]{1,0:T(8,128)S(1)} %shard_map.37) | data formatting | bytes 16777216
  (8 shorter events, 0.1 us)
Async XLA Ops:
  0.0 3.3 %copy-start = (bf16[4096,256]{1,0:T(8,128)(2,1)S(1)}, bf16[4096,256]{1,0:T(8,128)(2,1)}, u32[]{:S(2)}) copy-start(bf16[4096,256]{1,0:T(8,128)(2,1)} %param.4) | copy-start | bytes 6291460
  12.3 33.1 %all-to-all-start.1 = ((bf16[8,256,256]{2,1,0:T(8,128)(2,1)}), bf16[8,256,256]{2,1,0:T(8,128)(2,1)S(1)}, u32[]{:S(2)}, u32[]{:S(2)}) async-start(bf16[8,256,256]{2,1,0:T(8,128)(2,1)} %bitcast.22), calls=%async_computation.1 | async-start | bytes 2097152 | tf_op jit(solution)/shard_map/all_to_all | solution.py:250
  45.4 52.1 %all-to-all-start = ((bf16[8,256,512]{2,1,0:T(8,128)(2,1)}), bf16[8,256,512]{2,1,0:T(8,128)(2,1)}, u32[]{:S(2)}, u32[]{:S(2)}) async-start(bf16[8,256,512]{2,1,0:T(8,128)(2,1)} %bitcast.21), calls=%async_computation | async-start | bytes 4194304 | tf_op jit(solution)/shard_map/all_to_all | solution.py:250
